TPU v7x, 32 devices: a whole 2x2x4 slice. The times are simulated.
32 devices in a mesh: branch: 16 (over z, y, core), head: 2 (over x).
Axes of the slice: x: 2, y: 2, z: 4, core: 2. Of those that a mesh axis runs over, the one named last changes fastest.
Arguments:
- queries: bfloat16 [16, 256, 64, 128], P('branch', None, 'head'), may hold values from -8 to 8
- grad_out: bfloat16 [16, 256, 64, 128], P('branch', None, 'head'), may hold values from -6 to 6
- branch_keys: bfloat16 [16, 256, 8, 128], P('branch', None, 'head'), may hold values from -8 to 8
- branch_values: bfloat16 [16, 256, 8, 128], P('branch', None, 'head'), may hold values from -6 to 6
- row_lse: float32 [16, 64, 256], P('branch', 'head'), may hold values from -100 to 100, as said below
- row_delta: float32 [16, 64, 256], P('branch', 'head'), may hold values from -36 to 36
- lengths: int32 [16], P('branch'), may hold values from 128 to 256, as said below
- prompt_keys: bfloat16 [512, 8, 128], P(('branch', 'head')), may hold values from -8 to 8
- prompt_values: bfloat16 [512, 8, 128], P(('branch', 'head')), may hold values from -6 to 6
Outputs:
- query_grads: bfloat16 [16, 256, 64, 128], P('branch', None, 'head')
- branch_dkey: bfloat16 [16, 256, 8, 128], P('branch', None, 'head')
- branch_dvalue: bfloat16 [16, 256, 8, 128], P('branch', None, 'head')
- prompt_dkey: bfloat16 [512, 8, 128], P(('branch', 'head'))
- prompt_dvalue: bfloat16 [512, 8, 128], P(('branch', 'head'))
Inputs may be any that keep to these rules, and one draw needn't show every extreme that they name: row_lse[b, h, i] is the logarithm of the sum of exp(scaling * queries[b, i, h] . K_b[t, group of h]) over all t < 512 + i + 1, whatever the branch's length. `lengths`: some branch has exactly 256 valid positions and some exactly 128.
All inputs are finite; a program needn't handle non-finite values.
Results may differ from a plain program's by a relative error of at most 0.008.
Values may be sent and summed in bfloat16 or wider, within the bound.
A program may use at most 64 MiB of HBM per device.

v0:
```python
import math

import jax
import jax.numpy as jnp
from jax import lax
from jax.sharding import PartitionSpec as P


def score_pieces(queries, grad_out, lse_rows, delta_rows, key_rows, value_rows, visible, scaling):
    scores = (
        jnp.einsum("sgrd,kgd->grsk", queries, key_rows, preferred_element_type=jnp.float32)
        * scaling
    )
    weights = jnp.where(visible, jnp.exp(scores - lse_rows[..., None]), 0.0)
    weights_low = weights.astype(jnp.bfloat16)
    weight_grad = jnp.einsum(
        "sgrd,kgd->grsk", grad_out, value_rows, preferred_element_type=jnp.float32
    )
    score_grad = (weights * (weight_grad - delta_rows[..., None])).astype(jnp.bfloat16)
    query_grad = (
        jnp.einsum("grsk,kgd->sgrd", score_grad, key_rows, preferred_element_type=jnp.float32)
        * scaling
    )
    return (query_grad, weights_low, score_grad)


def edge_grads(weights_low, score_grad, queries, grad_out, scaling):
    value_grad = jnp.einsum(
        "grsk,sgrd->kgd", weights_low, grad_out, preferred_element_type=jnp.float32
    )
    key_grad = (
        jnp.einsum("grsk,sgrd->kgd", score_grad, queries, preferred_element_type=jnp.float32)
        * scaling
    )
    return (key_grad, value_grad)


def block_size():
    return 256


def regroup(rows, outer, inner):
    shaped = rows.reshape((outer, inner, rows.shape[0] // (outer * inner)) + rows.shape[1:])
    return jnp.swapaxes(shaped, 0, 1).reshape(rows.shape)


def shards(
    queries,
    grad_out,
    branch_keys,
    branch_values,
    row_lse,
    row_delta,
    lengths,
    prompt_keys,
    prompt_values,
):
    seq_len = queries.shape[1]
    head_count = queries.shape[2]
    head_dim = queries.shape[3]
    groups = branch_keys.shape[2]
    group_size = head_count // groups
    scaling = 1.0 / math.sqrt(head_dim)
    branch_count = lax.axis_size("branch")
    head_devices = lax.axis_size("head")
    query_grouped = queries[0].reshape(seq_len, groups, group_size, head_dim)
    grad_grouped = grad_out[0].reshape(seq_len, groups, group_size, head_dim)
    lse_rows = row_lse[0].reshape(groups, group_size, seq_len)
    delta_rows = row_delta[0].reshape(groups, group_size, seq_len)
    positions = lax.iota(jnp.int32, seq_len)
    live_rows = positions < lengths[0]
    wide_keys, wide_values = (
        lax.all_gather(prompt_keys, "branch", axis=0, tiled=True),
        lax.all_gather(prompt_values, "branch", axis=0, tiled=True),
    )
    mixed_keys, mixed_values = (
        lax.all_to_all(wide_keys, "head", split_axis=1, concat_axis=0, tiled=True),
        lax.all_to_all(wide_values, "head", split_axis=1, concat_axis=0, tiled=True),
    )
    cache_keys = regroup(mixed_keys, head_devices, branch_count)
    cache_values = regroup(mixed_values, head_devices, branch_count)
    query_total = jnp.zeros((seq_len, groups, group_size, head_dim), jnp.float32)
    prompt_len = cache_keys.shape[0]
    prompt_block = block_size()
    prompt_visible = live_rows[:, None]
    low_parts = []
    grad_parts = []
    for offset in range(0, prompt_len, prompt_block):
        query_part, weights_low, score_grad = score_pieces(
            query_grouped,
            grad_grouped,
            lse_rows,
            delta_rows,
            cache_keys[offset : offset + prompt_block],
            cache_values[offset : offset + prompt_block],
            prompt_visible,
            scaling,
        )
        query_total = query_total + query_part
        low_parts.append(weights_low)
        grad_parts.append(score_grad)
    branch_block = block_size()
    offset = 0
    key_positions = offset + lax.iota(jnp.int32, branch_block)
    visible = live_rows[:, None] & (key_positions[None, :] <= positions[:, None])
    query_part, weights_low, score_grad = score_pieces(
        query_grouped,
        grad_grouped,
        lse_rows,
        delta_rows,
        branch_keys[0, offset : offset + branch_block],
        branch_values[0, offset : offset + branch_block],
        visible,
        scaling,
    )
    key_part, value_part = edge_grads(weights_low, score_grad, query_grouped, grad_grouped, scaling)
    query_total = query_total + query_part
    own_dkey = key_part.astype(jnp.bfloat16)
    own_dvalue = value_part.astype(jnp.bfloat16)
    stored_low = jnp.concatenate(low_parts, 3)
    stored_grad = jnp.concatenate(grad_parts, 3)
    key_term, value_term = edge_grads(stored_low, stored_grad, query_grouped, grad_grouped, scaling)
    summed = lax.psum_scatter(
        jnp.stack([key_term, value_term], 1), "branch", scatter_dimension=0, tiled=True
    )
    prompt_dkey, prompt_dvalue = (
        lax.all_to_all(
            summed[:, 0].astype(jnp.bfloat16), "head", split_axis=0, concat_axis=1, tiled=True
        ),
        lax.all_to_all(
            summed[:, 1].astype(jnp.bfloat16), "head", split_axis=0, concat_axis=1, tiled=True
        ),
    )
    query_grads = query_total.reshape(seq_len, head_count, head_dim).astype(jnp.bfloat16)[None]
    branch_dkey = own_dkey[None]
    branch_dvalue = own_dvalue[None]
    return (query_grads, branch_dkey, branch_dvalue, prompt_dkey, prompt_dvalue)


def solution(mesh):
    in_specs = (
        P("branch", None, "head", None),
        P("branch", None, "head", None),
        P("branch", None, "head", None),
        P("branch", None, "head", None),
        P("branch", "head", None),
        P("branch", "head", None),
        P("branch"),
        P(("branch", "head"), None, None),
        P(("branch", "head"), None, None),
    )
    out_specs = (
        P("branch", None, "head", None),
        P("branch", None, "head", None),
        P("branch", None, "head", None),
        P(("branch", "head"), None, None),
        P(("branch", "head"), None, None),
    )
    return jax.shard_map(shards, mesh=mesh, in_specs=in_specs, out_specs=out_specs, check_vma=False)
```

profile of v0, /device:TPU:0, one launch (start us, length us, event | category | flops | bytes accessed | tf_op | source)
XLA Modules:
  0.0 189.6 jit_solution(6986431483613532422)
XLA Ops:
  7.2 0.0 copy-start
  7.2 25.0 %all_gather.6 = bf16[256,8,128]{2,1,0:T(8,128)(2,1)S(1)} all-gather(bf16[16,8,128]{2,1,0:T(8,128)(2,1)} %param.16), channel_id=1, replica_groups=mesh['branch'=16,'head'=2] {'branch'}, dimensions={0}, use_global_device_ids=true | all-gather | bytes 557056 | tf_op jit(solution)/shard_map/all_gather | solution.py:73
  32.1 0.9 copy.62
  33.0 3.5 %all-to-all-start = ((bf16[256,8,128]{2,0,1:T(8,128)(2,1)}), bf16[256,8,128]{2,0,1:T(8,128)(2,1)S(1)}, u32[]{:S(2)}, u32[]{:S(2)}) async-start(bf16[256,8,128]{2,0,1:T(8,128)(2,1)} %copy.62), calls=%async_computation | async-start | bytes 1048576 | tf_op jit(solution)/shard_map/all_to_all | solution.py:77
  37.2 19.1 %all_gather.7 = bf16[256,8,128]{2,1,0:T(8,128)(2,1)S(1)} all-gather(bf16[16,8,128]{2,1,0:T(8,128)(2,1)} %param.17), channel_id=1, replica_groups=mesh['branch'=16,'head'=2] {'branch'}, dimensions={0}, use_global_device_ids=true | all-gather | bytes 557056 | tf_op jit(solution)/shard_map/all_gather | solution.py:74
  56.3 0.9 copy.65
  57.2 0.0 all-to-all-done
  57.2 3.5 %all-to-all-start.1 = ((bf16[256,8,128]{2,0,1:T(8,128)(2,1)}), bf16[256,8,128]{2,0,1:T(8,128)(2,1)S(1)}, u32[]{:S(2)}, u32[]{:S(2)}) async-start(bf16[256,8,128]{2,0,1:T(8,128)(2,1)} %copy.65), calls=%async_computation.1 | async-start | bytes 1048576 | tf_op jit(solution)/shard_map/all_to_all | solution.py:78
  60.7 0.0 reduce-scatter.2.cloned.1.call-start
  60.8 0.0 copy-start.6
  60.9 0.0 copy-start.8
  60.9 8.7 %all-to-all-done.1 = bf16[256,8,128]{2,0,1:T(8,128)(2,1)S(1)} async-done(((bf16[256,8,128]{2,0,1:T(8,128)(2,1)}), bf16[256,8,128]{2,0,1:T(8,128)(2,1)S(1)}, u32[]{:S(2)}, u32[]{:S(2)}) %all-to-all-start.1) | async-done | bytes 524320 | tf_op jit(solution)/shard_map/all_to_all | solution.py:78
  69.6 0.7 copy.66
  70.3 0.0 copy-done
  70.3 0.0 copy-start.12
  70.4 1.4 fusion.59
  71.7 0.0 copy-done.6
  71.7 0.0 copy-done.8
  71.7 0.0 copy-done.12
  71.8 0.0 copy-start.13
  71.8 0.0 copy-start.16
  71.8 5.7 %fusion.20 = (bf16[4,8,256,256]{2,3,1,0:T(8,128)(2,1)}, bf16[4,8,256,256]{2,3,1,0:T(8,128)(2,1)}, f32[4,256,256,8]{2,1,3,0:T(8,128)S(1)}) fusion(f32[4,8,256]{2,1,0:T(8,128)S(1)} %bitcast.187, pred[256]{0:T(512)(128)(4,1)S(1)} %iota_compare_fusion.1, f32[4,256,256,8]{2,1,3,0:T(8,128)S(1)} %fusion.59, bf16[256,4,128,1]{2,0,3,1:T(8,128)(2,1)S(1)} %bitcast.177, ...), kind=kOutput, calls=%fused_computation.26 | convolution fusion | flops 553648128 | bytes 27558144 | tf_op jit(solution)/shard_map/sgrd,kgd->grsk/dot_general | solution.py:11
  77.4 0.0 copy-done.13
  77.4 0.0 copy-done.16
  77.4 3.2 %fusion.13 = bf16[4,8,256,256]{2,3,1,0:T(8,128)(2,1)S(1)} fusion(f32[4,256,256,8]{2,1,3,0:T(8,128)S(1)} %fusion.59, f32[4,8,256]{2,1,0:T(8,128)S(1)} %bitcast.200, f32[4,8,256]{2,1,0:T(8,128)S(1)} %bitcast.188, pred[256]{0:T(512)(128)(4,1)S(1)} %iota_compare_fusion.1, bf16[256,4,128,1]{2,0,3,1:T(8,128)(2,1)S(1)} %bitcast.184, ...), kind=kOutput, calls=%fused_computation.16 | convolution fusion | flops 549453824 | bytes 15008000 | tf_op jit(solution)/shard_map/sgrd,kgd->grsk/dot_general | solution.py:16
  80.6 0.0 copy-start.2
  80.6 0.0 copy-done.11
  80.7 7.1 %fusion.17 = bf16[4,8,256,256]{2,3,1,0:T(8,128)(2,1)S(1)} fusion(f32[4,256,256,8]{2,1,3,0:T(8,128)S(1)} %get-tuple-element.28, f32[4,8,256]{2,1,0:T(8,128)S(1)} %bitcast.201, f32[4,8,256]{2,1,0:T(8,128)S(1)} %bitcast.189, pred[256]{0:T(512)(128)(4,1)S(1)} %iota_compare_fusion.1, bf16[256,4,128,1]{2,0,3,1:T(8,128)(2,1)S(1)} %bitcast.183, ...), kind=kOutput, calls=%fused_computation.22 | convolution fusion | flops 549453824 | bytes 15008000 | tf_op jit(solution)/shard_map/sgrd,kgd->grsk/dot_general | solution.py:16
  87.8 0.0 copy-done.2
  87.8 0.0 copy-start.3
  87.8 0.0 copy-start.5
  87.8 3.2 %fusion.35 = f32[512,1,4,128]{3,0,2,1:T(8,128)S(1)} fusion(bf16[4,8,256,256]{2,3,1,0:T(8,128)(2,1)S(1)} %fusion.13, bf16[4,8,256,256]{2,3,1,0:T(8,128)(2,1)S(1)} %fusion.17, bf16[256,4,8,128]{3,2,1,0:T(8,128)(2,1)S(1)} %bitcast.170), kind=kOutput, calls=%fused_computation.36 | convolution fusion | flops 1090781184 | bytes 11534336 | tf_op jit(solution)/shard_map/grsk,sgrd->kgd/dot_general | solution.py:32
  91.0 0.0 copy-done.3
  91.1 0.5 copy-done.5
  91.5 5.3 %fusion.26 = f32[512,1,4,128]{3,0,2,1:T(8,128)S(1)} fusion(bf16[4,8,256,256]{2,3,1,0:T(8,128)(2,1)} %get-tuple-element.27, bf16[4,8,256,256]{2,3,1,0:T(8,128)(2,1)S(1)} %copy-done.5, bf16[256,4,8,128]{3,2,1,0:T(8,128)(2,1)} %bitcast.195), kind=kOutput, calls=%fused_computation.33 | convolution fusion | flops 1090519040 | bytes 11534336 | tf_op jit(solution)/shard_map/grsk,sgrd->kgd/dot_general | solution.py:28
  96.8 0.0 copy-start.10
  96.8 1.5 pad_maximum_fusion
  98.3 0.0 reduce-scatter.2.cloned.1.call-update
  98.3 0.0 copy-done.10
  98.3 0.0 copy-start.14
  98.4 0.0 copy-start.15
  98.4 1.4 fusion.57
  99.7 0.2 copy-done.14
  99.9 0.0 copy-done.15
  99.9 3.6 %fusion.9 = bf16[4,8,256,256]{2,3,1,0:T(8,128)(2,1)S(1)} fusion(f32[4,256,256,8]{2,1,3,0:T(8,128)S(1)} %fusion.57, f32[4,8,256]{2,1,0:T(8,128)S(1)} %bitcast.202, f32[4,8,256]{2,1,0:T(8,128)S(1)} %bitcast.190, pred[256,256]{0,1:T(8,128)(4,1)S(1)} %fusion.64, bf16[256,4,8,128]{3,2,1,0:T(8,128)(2,1)S(1)} %bitcast.197, bf16[256,4,128,1]{2,1,0,3:T(4,128)(2,1)S(1)} %bitcast.199), kind=kOutput, calls=%fused_computation.10 | convolution fusion | flops 549453824 | bytes 15073280 | tf_op jit(solution)/shard_map/sgrd,kgd->grsk/dot_general | solution.py:16
  103.6 1.5 fusion.46
  105.0 0.9 copy.89
  105.9 2.4 %fusion.47 = bf16[1,256,4,128]{3,1,2,0:T(8,128)(2,1)S(1)} fusion(f32[4,256,256,8]{2,1,3,0:T(8,128)S(1)} %fusion.57, f32[4,8,256]{2,1,0:T(8,128)S(1)} %bitcast.191, pred[256,256]{0,1:T(8,128)(4,1)S(1)} %fusion.64, bf16[256,4,8,128]{3,2,1,0:T(8,128)(2,1)S(1)} %bitcast.198), kind=kOutput, calls=%fused_computation.43 | convolution fusion | flops 545390592 | bytes 10846208 | tf_op jit(solution)/shard_map/grsk,sgrd->kgd/dot_general | solution.py:28
  108.3 0.9 copy.90
  109.2 0.0 copy-done.9
  109.3 3.7 %fusion.73 = f32[4,8,256,128]{3,2,1,0:T(8,128)} fusion(bf16[4,8,256,256]{2,3,1,0:T(8,128)(2,1)S(1)} %copy-done.4, bf16[256,4,128,1]{2,0,3,1:T(8,128)(2,1)S(1)} %bitcast.178), kind=kOutput, calls=%fused_computation.71 | convolution fusion | flops 536870912 | bytes 8650752 | tf_op jit(solution)/shard_map/grsk,kgd->sgrd/dot_general | solution.py:21
  112.9 44.9 %reduce-scatter.2.cloned.1.call-done = f32[32,2,4,128]{3,0,2,1:T(8,128)} async-done(((f32[512,2,4,128]{3,0,2,1:T(8,128)}), f32[32,2,4,128]{3,0,2,1:T(8,128)}) %reduce-scatter.2.cloned.1.call-update) | async-done | bytes 131088 | tf_op jit(solution)/shard_map/reduce_scatter | solution.py:123
  157.8 0.9 convert.4
  158.8 0.6 copy.84
  159.4 3.3 %all-to-all-start.2 = ((bf16[32,4,128]{2,1,0:T(4,128)(2,1)}), bf16[32,4,128]{2,1,0:T(4,128)(2,1)S(1)}, u32[]{:S(2)}, u32[]{:S(2)}) async-start(bf16[32,4,128]{2,1,0:T(4,128)(2,1)} %copy.84), calls=%async_computation.3 | async-start | bytes 65536 | tf_op jit(solution)/shard_map/all_to_all | solution.py:127
  162.7 5.8 %fusion.74 = f32[4,8,256,128]{3,2,1,0:T(8,128)} fusion(bf16[4,8,256,256]{2,3,1,0:T(8,128)(2,1)} %copy-done.2, bf16[256,4,128,1]{2,0,3,1:T(8,128)(2,1)S(1)} %bitcast.176), kind=kOutput, calls=%fused_computation.72 | convolution fusion | flops 536870912 | bytes 8650752 | tf_op jit(solution)/shard_map/grsk,kgd->sgrd/dot_general | solution.py:21
  168.5 0.6 copy.86
  169.1 0.0 all-to-all-done.2
  169.1 3.3 %all-to-all-start.3 = ((bf16[32,4,128]{2,1,0:T(4,128)(2,1)}), bf16[32,4,128]{2,1,0:T(4,128)(2,1)S(1)}, u32[]{:S(2)}, u32[]{:S(2)}) async-start(bf16[32,4,128]{2,1,0:T(4,128)(2,1)} %copy.86), calls=%async_computation.4 | async-start | bytes 65536 | tf_op jit(solution)/shard_map/all_to_all | solution.py:130
  172.4 6.5 %multiply_convert_fusion = bf16[4,8,256,128]{3,2,1,0:T(8,128)(2,1)S(1)} fusion(f32[4,8,256,128]{3,2,1,0:T(8,128)} %fusion.73, f32[4,8,256,128]{3,2,1,0:T(8,128)} %fusion.74, bf16[4,8,256,256]{2,3,1,0:T(8,128)(2,1)} %copy-done.1, bf16[256,4,128,1]{2,1,0,3:T(4,128)(2,1)S(1)} %bitcast.182), kind=kOutput, calls=%fused_computation.29 | convolution fusion | flops 541065216 | bytes 14942208 | tf_op jit(solution)/shard_map/grsk,kgd->sgrd/dot_general | solution.py:21
  178.9 2.7 %copy.88 = bf16[1,256,32,128]{3,2,1,0:T(8,128)(2,1)} copy(bf16[1,256,32,128]{3,1,2,0:T(8,128)(2,1)S(1)} %bitcast.174) | data formatting | bytes 4194304
  181.5 0.6 copy.85
  182.2 0.0 all-to-all-done.3
  182.2 0.6 copy.87
  (16 shorter events, 0.2 us)
Async XLA Ops:
  7.2 63.2 %copy-start = (bf16[1,256,32,128]{3,2,1,0:T(8,128)(2,1)S(1)}, bf16[1,256,32,128]{3,2,1,0:T(8,128)(2,1)}, u32[]{:S(2)}) copy-start(bf16[1,256,32,128]{3,2,1,0:T(8,128)(2,1)} %param.9) | copy-start | bytes 6291460
  33.0 24.2 %all-to-all-start = ((bf16[256,8,128]{2,0,1:T(8,128)(2,1)}), bf16[256,8,128]{2,0,1:T(8,128)(2,1)S(1)}, u32[]{:S(2)}, u32[]{:S(2)}) async-start(bf16[256,8,128]{2,0,1:T(8,128)(2,1)} %copy.62), calls=%async_computation | async-start | bytes 1048576 | tf_op jit(solution)/shard_map/all_to_all | solution.py:77
  57.2 12.4 %all-to-all-start.1 = ((bf16[256,8,128]{2,0,1:T(8,128)(2,1)}), bf16[256,8,128]{2,0,1:T(8,128)(2,1)S(1)}, u32[]{:S(2)}, u32[]{:S(2)}) async-start(bf16[256,8,128]{2,0,1:T(8,128)(2,1)} %copy.65), calls=%async_computation.1 | async-start | bytes 1048576 | tf_op jit(solution)/shard_map/all_to_all | solution.py:78
  60.7 97.2 %reduce-scatter.2.cloned.1.call-start = ((), (), s32[]{:S(2)}) async-start(), calls=%async_computation.5 | async-start | bytes 2228224 | tf_op jit(solution)/shard_map/reduce_scatter | solution.py:123
  60.8 10.9 %copy-start.6 = (bf16[8,2,16,4,128]{4,2,1,0,3:T(8,128)(2,1)}, bf16[8,2,16,4,128]{4,2,1,0,3:T(8,128)(2,1)S(1)}, u32[]{:S(2)}) copy-start(bf16[8,2,16,4,128]{4,2,1,0,3:T(8,128)(2,1)S(1)} %copy.69) | copy-start | bytes 786436
  60.9 10.9 %copy-start.8 = (bf16[8,2,16,4,128]{4,2,1,0,3:T(8,128)(2,1)}, bf16[8,2,16,4,128]{4,2,1,0,3:T(8,128)(2,1)S(1)}, u32[]{:S(2)}) copy-start(bf16[8,2,16,4,128]{4,2,1,0,3:T(8,128)(2,1)S(1)} %copy.63) | copy-start | bytes 786436
  70.3 1.4 copy-start.12
  71.8 5.7 %copy-start.13 = (bf16[1,256,32,128]{3,2,1,0:T(8,128)(2,1)S(1)}, bf16[1,256,32,128]{3,2,1,0:T(8,128)(2,1)}, u32[]{:S(2)}) copy-start(bf16[1,256,32,128]{3,2,1,0:T(8,128)(2,1)} %param.10) | copy-start | bytes 6291460
  71.8 5.7 %copy-start.16 = (f32[1,32,256]{2,1,0:T(8,128)S(1)}, f32[1,32,256]{2,1,0:T(8,128)}, u32[]{:S(2)}) copy-start(f32[1,32,256]{2,1,0:T(8,128)} %param.14) | copy-start | bytes 98308
  77.4 3.2 %copy-start.11 = (bf16[8,2,16,4,128]{4,2,1,0,3:T(8,128)(2,1)S(1)}, bf16[8,2,16,4,128]{4,2,1,0,3:T(8,128)(2,1)}, u32[]{:S(2)}) copy-start(bf16[8,2,16,4,128]{4,2,1,0,3:T(8,128)(2,1)} %copy.66) | copy-start | bytes 786436
  80.6 7.2 %copy-start.2 = (bf16[4,8,256,256]{2,3,1,0:T(8,128)(2,1)}, bf16[4,8,256,256]{2,3,1,0:T(8,128)(2,1)S(1)}, u32[]{:S(2)}) copy-start(bf16[4,8,256,256]{2,3,1,0:T(8,128)(2,1)S(1)} %fusion.13) | copy-start | bytes 12582916
  87.8 3.2 %copy-start.3 = (bf16[4,8,256,256]{2,3,1,0:T(8,128)(2,1)}, bf16[4,8,256,256]{2,3,1,0:T(8,128)(2,1)S(1)}, u32[]{:S(2)}) copy-start(bf16[4,8,256,256]{2,3,1,0:T(8,128)(2,1)S(1)} %fusion.17) | copy-start | bytes 12582916
  87.8 3.7 %copy-start.5 = (bf16[4,8,256,256]{2,3,1,0:T(8,128)(2,1)S(1)}, bf16[4,8,256,256]{2,3,1,0:T(8,128)(2,1)}, u32[]{:S(2)}) copy-start(bf16[4,8,256,256]{2,3,1,0:T(8,128)(2,1)} %get-tuple-element.26) | copy-start | bytes 12582916
  96.8 1.5 copy-start.10
  98.3 1.6 copy-start.14
  98.4 1.6 copy-start.15
  103.6 4.8 %copy-start.1 = (bf16[4,8,256,256]{2,3,1,0:T(8,128)(2,1)}, bf16[4,8,256,256]{2,3,1,0:T(8,128)(2,1)S(1)}, u32[]{:S(2)}) copy-start(bf16[4,8,256,256]{2,3,1,0:T(8,128)(2,1)S(1)} %fusion.9) | copy-start | bytes 12582916
  105.9 3.3 %copy-start.4 = (bf16[4,8,256,256]{2,3,1,0:T(8,128)(2,1)S(1)}, bf16[4,8,256,256]{2,3,1,0:T(8,128)(2,1)}, u32[]{:S(2)}) copy-start(bf16[4,8,256,256]{2,3,1,0:T(8,128)(2,1)} %copy-done.3) | copy-start | bytes 12582916
  105.9 3.3 %copy-start.9 = (bf16[8,2,16,4,128]{4,2,1,0,3:T(8,128)(2,1)S(1)}, bf16[8,2,16,4,128]{4,2,1,0,3:T(8,128)(2,1)}, u32[]{:S(2)}) copy-start(bf16[8,2,16,4,128]{4,2,1,0,3:T(8,128)(2,1)} %copy-done.8) | copy-start | bytes 786436
  109.2 53.4 %copy-start.7 = (bf16[8,2,16,4,128]{4,2,1,0,3:T(8,128)(2,1)S(1)}, bf16[8,2,16,4,128]{4,2,1,0,3:T(8,128)(2,1)}, u32[]{:S(2)}) copy-start(bf16[8,2,16,4,128]{4,2,1,0,3:T(8,128)(2,1)} %copy-done.6) | copy-start | bytes 786436
  159.4 9.7 %all-to-all-start.2 = ((bf16[32,4,128]{2,1,0:T(4,128)(2,1)}), bf16[32,4,128]{2,1,0:T(4,128)(2,1)S(1)}, u32[]{:S(2)}, u32[]{:S(2)}) async-start(bf16[32,4,128]{2,1,0:T(4,128)(2,1)} %copy.84), calls=%async_computation.3 | async-start | bytes 65536 | tf_op jit(solution)/shard_map/all_to_all | solution.py:127
  169.1 13.1 %all-to-all-start.3 = ((bf16[32,4,128]{2,1,0:T(4,128)(2,1)}), bf16[32,4,128]{2,1,0:T(4,128)(2,1)S(1)}, u32[]{:S(2)}, u32[]{:S(2)}) async-start(bf16[32,4,128]{2,1,0:T(4,128)(2,1)} %copy.86), calls=%async_computation.4 | async-start | bytes 65536 | tf_op jit(solution)/shard_map/all_to_all | solution.py:130
Sparse Core Ops, SparseCore 0:
  98.4 59.3 reduce-scatter.1
where the time goes:
time: 190 us
  waiting for transfers between devices  53.6 us (28%)
  matrix products  50.6 us (27%)
  blocking collectives  44.1 us (23%)
  between operations  15 us (8%)
  starting transfers between devices  13.5 us (7%)
  local copies, waits for them, and re-layouts  10.4 us (5%)
  other arithmetic  2.42 us (1%)
    reduce_scatter x1, waiting for transfers between devices, shards(): lax.psum_scatter(jnp.stack([key_term, value_term], 1), 'branch', scatter_...  44.9 us
    all_gather x1, blocking collectives, shards(): lax.all_gather(prompt_keys, 'branch', axis=0, tiled=True)  25 us
    all_gather x1, blocking collectives, shards(): lax.all_gather(prompt_values, 'branch', axis=0, tiled=True)  19.1 us
    dot_general x3, matrix products, score_pieces(): jnp.einsum('grsk,kgd->sgrd', score_grad, key_rows, preferred_element_type...  16 us
    dot_general x3, matrix products, score_pieces(): jnp.einsum('sgrd,kgd->grsk', grad_out, value_rows, preferred_element_type...  13.9 us
    all_to_all x1, waiting for transfers between devices, shards(): lax.all_to_all(wide_values, 'head', split_axis=1, concat_axis=0, tiled=True)  8.67 us
    dot_general x3, matrix products, score_pieces(): jnp.einsum('sgrd,kgd->grsk', queries, key_rows, preferred_element_type=jn...  8.38 us
    dot_general x2, matrix products, edge_grads(): jnp.einsum('grsk,sgrd->kgd', weights_low, grad_out, preferred_element_typ...  7.64 us
  transfers between devices with their start and end apart: 5, of which 2 were waited for; matrix products, arithmetic and copies ran while one was open for 17% of the time, Pallas kernels for 0%

commit v1 on v0

--- a/solution.py
+++ b/solution.py
@@ -1,8 +1,11 @@
+import functools
 import math
 
 import jax
 import jax.numpy as jnp
 from jax import lax
+from jax.experimental import pallas as pl
+from jax.experimental.pallas import tpu as pltpu
 from jax.sharding import PartitionSpec as P
 
 
@@ -44,7 +47,7 @@
     return jnp.swapaxes(shaped, 0, 1).reshape(rows.shape)
 
 
-def shards(
+def plain_shards(
     queries,
     grad_out,
     branch_keys,
@@ -137,6 +140,303 @@
     return (query_grads, branch_dkey, branch_dvalue, prompt_dkey, prompt_dvalue)
 
 
+MESH = pl.DeviceIdType.MESH
+LOG2E = math.log2(math.e)
+NT = (((1,), (1,)), ((), ()))
+
+
+def block_terms(q, do, lse, delta, k, v, k_t, keep, score_scale):
+    s = lax.dot_general(k, q, NT, preferred_element_type=jnp.float32)
+    p = jnp.exp2(s * score_scale - lse)
+    if keep is not None:
+        p = jnp.where(keep, p, 0.0)
+    dp = lax.dot_general(v, do, NT, preferred_element_type=jnp.float32)
+    ds = (p * (dp - delta)).astype(jnp.bfloat16)
+    dv = jnp.dot(p.astype(jnp.bfloat16), do, preferred_element_type=jnp.float32)
+    dk = jnp.dot(ds, q, preferred_element_type=jnp.float32)
+    dq_t = jnp.dot(k_t, ds, preferred_element_type=jnp.float32)
+    return dq_t, dk, dv
+
+
+def fused_kernel(
+    dims,
+    q_hbm,
+    do_hbm,
+    bk_ref,
+    bv_ref,
+    rows_ref,
+    packed_ref,
+    dq_hbm,
+    bdk_ref,
+    bdv_ref,
+    pd_ref,
+    q_scr,
+    do_scr,
+    dq_acc,
+    dq_scr,
+    dk_acc,
+    dv_acc,
+    kt_scr,
+    gath,
+    send,
+    recv,
+    load_sem,
+    store_sem,
+    gather_sem,
+    own_sem,
+    scatter_send_sem,
+    scatter_recv_sem,
+):
+    branch_count, head_devices, groups, group_size, seq_len, head_dim, pos = dims
+    devices = branch_count * head_devices
+    prompt_len = devices * pos
+    scaling = 1.0 / math.sqrt(head_dim)
+    score_scale = scaling * LOG2E
+    rows = seq_len * group_size
+    wide = 64 * group_size
+    chunk = 256
+    early = groups // 2
+    me = lax.axis_index("branch") * head_devices + lax.axis_index("head")
+
+    def ident(index):
+        return (index // head_devices, index % head_devices)
+
+    def loads(g):
+        cut = pl.ds(g * group_size, group_size)
+        return (
+            pltpu.make_async_copy(q_hbm.at[0, :, cut, :], q_scr.at[g], load_sem.at[0, g]),
+            pltpu.make_async_copy(do_hbm.at[0, :, cut, :], do_scr.at[g], load_sem.at[1, g]),
+        )
+
+    for g in range(groups):
+        for copy in loads(g):
+            copy.start()
+
+    barrier = pltpu.get_barrier_semaphore()
+
+    @pl.loop(1, devices)
+    def _(k):
+        pl.semaphore_signal(
+            barrier, inc=1, device_id=ident((me + k) % devices), device_id_type=MESH
+        )
+
+    dq_acc[...] = jnp.zeros_like(dq_acc)
+    pl.semaphore_wait(barrier, devices - 1)
+
+    @pl.loop(1, devices)
+    def _(k):
+        other = (me + k) % devices
+        pltpu.make_async_remote_copy(
+            src_ref=packed_ref.at[other % head_devices],
+            dst_ref=gath.at[k],
+            send_sem=gather_sem.at[0],
+            recv_sem=gather_sem.at[1],
+            device_id=ident(other),
+            device_id_type=MESH,
+        ).start()
+
+    own = pltpu.make_async_copy(packed_ref.at[me % head_devices], gath.at[0], own_sem)
+    own.start()
+
+    def row_block(g, j):
+        cut = pl.ds(j * 64, 64)
+        q = q_scr[g, cut].reshape(wide, head_dim)
+        do = do_scr[g, cut].reshape(wide, head_dim)
+        return q, do, rows_ref[g, j, 0:1, :], rows_ref[g, j, 1:2, :]
+
+    def branch_part(g):
+        k_all = bk_ref[g]
+        v_all = bv_ref[g]
+        k_t_all = k_all.T
+        steps = seq_len // 64
+        for j in reversed(range(steps)):
+            seen = (j + 1) * 64
+            q, do, lse, delta = row_block(g, j)
+            key_at = lax.broadcasted_iota(jnp.int32, (seen, wide), 0)
+            row_at = lax.broadcasted_iota(jnp.int32, (seen, wide), 1) // group_size
+            dq_t, dk, dv = block_terms(
+                q, do, lse, delta, k_all[:seen], v_all[:seen], k_t_all[:, :seen],
+                key_at <= row_at + j * 64, score_scale,
+            )
+            dq_acc[g, j] += dq_t
+            if j == steps - 1:
+                dk_acc[0:seen] = dk
+                dv_acc[0:seen] = dv
+            else:
+                dk_acc[0:seen] += dk
+                dv_acc[0:seen] += dv
+        bdk_ref[g] = (dk_acc[0:seq_len] * scaling).astype(jnp.bfloat16)
+        bdv_ref[g] = dv_acc[0:seq_len].astype(jnp.bfloat16)
+
+    def prompt_part(g):
+        kt_scr[...] = gath[:, 0, g].reshape(prompt_len, head_dim).T
+        dk_acc[...] = jnp.zeros_like(dk_acc)
+        dv_acc[...] = jnp.zeros_like(dv_acc)
+        per = chunk // pos
+
+        @pl.loop(0, seq_len // 64)
+        def _(j):
+            q, do, lse, delta = row_block(g, j)
+            total = None
+            for c in range(prompt_len // chunk):
+                at = slice(c * chunk, (c + 1) * chunk)
+                k = gath[c * per : (c + 1) * per, 0, g].reshape(chunk, head_dim)
+                v = gath[c * per : (c + 1) * per, 1, g].reshape(chunk, head_dim)
+                dq_t, dk, dv = block_terms(
+                    q, do, lse, delta, k, v, kt_scr[:, at], None, score_scale
+                )
+                dk_acc[at] += dk
+                dv_acc[at] += dv
+                total = dq_t if total is None else total + dq_t
+            dq_acc[g, j] += total
+
+        send[g, :, 0] = (dk_acc[...] * scaling).astype(jnp.bfloat16).reshape(devices, pos, head_dim)
+        send[g, :, 1] = dv_acc[...].astype(jnp.bfloat16).reshape(devices, pos, head_dim)
+
+        @pl.loop(1, devices)
+        def _(k):
+            pltpu.make_async_remote_copy(
+                src_ref=send.at[g, k],
+                dst_ref=recv.at[g, k],
+                send_sem=scatter_send_sem.at[g],
+                recv_sem=scatter_recv_sem.at[g],
+                device_id=ident((me + devices - k) % devices),
+                device_id_type=MESH,
+            ).start()
+
+    def store(g):
+        cut = pl.ds(g * group_size, group_size)
+        return pltpu.make_async_copy(dq_scr.at[g], dq_hbm.at[0, :, cut, :], store_sem.at[g])
+
+    def finish(g):
+        for j in range(seq_len // 64):
+            dq_scr[g, j * 64 : (j + 1) * 64] = (
+                (dq_acc[g, j] * scaling).T.astype(jnp.bfloat16).reshape(64, group_size, head_dim)
+            )
+        store(g).start()
+
+    @pl.loop(0, early)
+    def _(g):
+        for copy in loads(g):
+            copy.wait()
+        branch_part(g)
+
+    own.wait()
+    rest = pl.ds(1, devices - 1)
+    pltpu.make_async_copy(gath.at[rest], gath.at[rest], gather_sem.at[1]).wait()
+
+    @pl.loop(0, groups)
+    def _(g):
+        @pl.when(g >= early)
+        def _():
+            for copy in loads(g):
+                copy.wait()
+
+        prompt_part(g)
+
+    @pl.loop(0, early)
+    def _(g):
+        finish(g)
+
+    @pl.loop(early, groups)
+    def _(g):
+        branch_part(g)
+        finish(g)
+
+    pltpu.make_async_copy(gath.at[rest], gath.at[rest], gather_sem.at[0]).wait()
+
+    @pl.loop(0, groups)
+    def _(g):
+        pltpu.make_async_copy(send.at[g, rest], send.at[g, rest], scatter_send_sem.at[g]).wait()
+        pltpu.make_async_copy(recv.at[g, rest], recv.at[g, rest], scatter_recv_sem.at[g]).wait()
+        for apart in range(head_devices):
+            owner = (me + apart) % head_devices
+            total = None
+            for k in range(apart, devices, head_devices):
+                piece = (send if k == 0 else recv)[g, k].astype(jnp.float32)
+                total = piece if total is None else total + piece
+            pd_ref[owner, g] = total.astype(jnp.bfloat16)
+        store(g).wait()
+
+
+def shards(
+    queries,
+    grad_out,
+    branch_keys,
+    branch_values,
+    row_lse,
+    row_delta,
+    lengths,
+    prompt_keys,
+    prompt_values,
+):
+    branch_count = lax.axis_size("branch")
+    head_devices = lax.axis_size("head")
+    devices = branch_count * head_devices
+    _, seq_len, head_count, head_dim = queries.shape
+    groups = branch_keys.shape[2]
+    group_size = head_count // groups
+    pos = prompt_keys.shape[0]
+    if pos % 16:
+        return plain_shards(
+            queries, grad_out, branch_keys, branch_values, row_lse, row_delta, lengths,
+            prompt_keys, prompt_values,
+        )
+    prompt_len = devices * pos
+    wide = 64 * group_size
+    steps = seq_len // 64
+    live = lax.iota(jnp.int32, seq_len) < lengths[0]
+    lse = jnp.where(live, row_lse[0] * LOG2E, 1e30)
+    rows = jnp.stack([lse, row_delta[0]])
+    rows = rows.reshape(2, groups, group_size, steps, 64)
+    rows = rows.transpose(1, 3, 0, 4, 2).reshape(groups, steps, 2, wide)
+    packed = jnp.stack([prompt_keys, prompt_values])
+    packed = packed.reshape(2, pos, head_devices, groups, head_dim).transpose(2, 0, 3, 1, 4)
+    dims = (branch_count, head_devices, groups, group_size, seq_len, head_dim, pos)
+    vmem = pl.BlockSpec(memory_space=pltpu.VMEM)
+    hbm = pl.BlockSpec(memory_space=pl.ANY)
+    low, full = jnp.bfloat16, jnp.float32
+    dq, bdk, bdv, pd = pl.pallas_call(
+        functools.partial(fused_kernel, dims),
+        out_shape=(
+            jax.ShapeDtypeStruct(queries.shape, low),
+            jax.ShapeDtypeStruct((groups, seq_len, head_dim), low),
+            jax.ShapeDtypeStruct((groups, seq_len, head_dim), low),
+            jax.ShapeDtypeStruct((head_devices, groups, 2, pos, head_dim), low),
+        ),
+        in_specs=[hbm, hbm, vmem, vmem, vmem, vmem],
+        out_specs=(hbm, vmem, vmem, vmem),
+        scratch_shapes=[
+            pltpu.VMEM((groups, seq_len, group_size, head_dim), low),
+            pltpu.VMEM((groups, seq_len, group_size, head_dim), low),
+            pltpu.VMEM((groups, steps, head_dim, wide), full),
+            pltpu.VMEM((groups, seq_len, group_size, head_dim), low),
+            pltpu.VMEM((prompt_len, head_dim), full),
+            pltpu.VMEM((prompt_len, head_dim), full),
+            pltpu.VMEM((head_dim, prompt_len), low),
+            pltpu.VMEM((devices, 2, groups, pos, head_dim), low),
+            pltpu.VMEM((groups, devices, 2, pos, head_dim), low),
+            pltpu.VMEM((groups, devices, 2, pos, head_dim), low),
+            pltpu.SemaphoreType.DMA((2, groups)),
+            pltpu.SemaphoreType.DMA((groups,)),
+            pltpu.SemaphoreType.DMA((2,)),
+            pltpu.SemaphoreType.DMA,
+            pltpu.SemaphoreType.DMA((groups,)),
+            pltpu.SemaphoreType.DMA((groups,)),
+        ],
+        compiler_params=pltpu.CompilerParams(collective_id=0, has_side_effects=True),
+    )(
+        queries,
+        grad_out,
+        branch_keys[0].swapaxes(0, 1),
+        branch_values[0].swapaxes(0, 1),
+        rows,
+        packed,
+    )
+    pd = pd.transpose(2, 3, 0, 1, 4).reshape(2, pos, head_devices * groups, head_dim)
+    return (dq, bdk.swapaxes(0, 1)[None], bdv.swapaxes(0, 1)[None], pd[0], pd[1])
+
+
 def solution(mesh):
     in_specs = (
         P("branch", None, "head", None),

time: 190 us -> 86 us (0.45)
  Pallas kernels: 0 us -> 67.8 us
  waiting for transfers between devices: 53.6 us -> 0 us
  matrix products: 50.6 us -> 0 us
  blocking collectives: 44.1 us -> 0 us
  between operations: 15 us -> 1.34 us
  starting transfers between devices: 13.5 us -> 0 us
  local copies, waits for them, and re-layouts: 10.4 us -> 14.9 us
    pallas_call x0 -> x1, Pallas kernels: none -> 67.8 us  [shards(): pl.pallas_call(functools.partial(fused_kernel, dims), out_shape=(jax.Shap...]
    dot_general x13 -> x0, matrix products: 50.6 us -> none  [the longest x3 16 us: score_pieces(): jnp.einsum('grsk,kgd->sgrd', score_grad, key_rows, preferred_element_type...]
    reduce_scatter x1 -> x0, waiting for transfers between devices: 44.9 us -> none  [shards(): lax.psum_scatter(jnp.stack([key_term, value_term], 1), 'branch', scatter_...]
    all_gather x2 -> x0, blocking collectives: 44.1 us -> none  [the longest x1 25 us: shards(): lax.all_gather(prompt_keys, 'branch', axis=0, tiled=True)]
    all_to_all x4 -> x0, starting transfers between devices: 13.5 us -> none  [the longest x1 3.49 us: shards(): lax.all_to_all(wide_keys, 'head', split_axis=1, concat_axis=0, tiled=True)]
    all_to_all x4 -> x0, waiting for transfers between devices: 8.68 us -> none  [the longest x1 8.67 us: shards(): lax.all_to_all(wide_values, 'head', split_axis=1, concat_axis=0, tiled=True)]
    unnamed x37 -> x7, local copies, waits for them, and re-layouts: 5.26 us -> 9.76 us
    another operation x2 -> x0, other arithmetic: 2.38 us -> none  [the longest x1 1.47 us: shards(): jnp.stack([key_term, value_term], 1)]
  transfers between devices with their start and end apart: 5 -> 0, of which waited for: 2 -> 0; matrix products, arithmetic and copies ran while one was open for 17% -> 0% of each run, Pallas kernels for 0% -> 0%
where the time goes in v1:
time: 86 us; the launch traced here: 85.4 us
  Pallas kernels  67.8 us (79%)
  local copies, waits for them, and re-layouts  14.9 us (17%)
  other arithmetic  1.42 us (2%)
  between operations  1.34 us (2%)
    pallas_call x1, Pallas kernels, shards(): pl.pallas_call(functools.partial(fused_kernel, dims), out_shape=(jax.Shap...  67.8 us
    unnamed x7, local copies, waits for them, and re-layouts  9.76 us
    transpose x1, local copies, waits for them, and re-layouts, shards(): branch_values[0].swapaxes(0, 1)  1.89 us

profile of v1, /device:TPU:0, one launch (start us, length us, event | category | flops | bytes accessed | tf_op | source)
XLA Modules:
  0.0 85.4 jit_solution(14615718404497645080)
XLA Ops:
  1.3 0.8 multiply_select_fusion
  2.1 0.1 stack.17
  2.2 0.8 copy.48
  2.9 0.8 copy.49
  3.7 0.6 maximum_bitcast_fusion.1.packed_ref
  4.3 0.8 stack.18
  5.2 1.9 %copy_bitcast_fusion = (bf16[4,256,128]{2,1,0:T(8,128)(2,1)}, bf16[4,256,128]{2,1,0:T(8,128)(2,1)}) fusion(bf16[1,256,4,128]{3,2,1,0:T(4,128)(2,1)} %param.12, bf16[1,256,4,128]{3,2,1,0:T(4,128)(2,1)} %param.11), kind=kLoop, calls=%fused_computation | loop fusion | bytes 1048576 | tf_op jit(solution)/shard_map/transpose | solution.py:432
  7.1 0.3 copy.47
  7.5 1.2 %reshape.31.rows_ref = f32[4,4,2,512]{3,2,1,0:T(2,128)} reshape(f32[4,4,2,64,8]{4,3,2,1,0:T(8,128)S(1)} %copy.47) | data formatting | bytes 131072 | tf_op jit(solution)/shard_map/reshape | solution.py:392
  8.6 67.8 %shard_map.128 = (bf16[1,256,32,128]{3,2,1,0:T(8,128)(2,1)}, bf16[4,256,128]{2,1,0:T(8,128)(2,1)}, bf16[4,256,128]{2,1,0:T(8,128)(2,1)}, bf16[2,4,2,16,128]{4,3,2,1,0:T(8,128)(2,1)}) custom-call(bf16[1,256,32,128]{3,2,1,0:T(8,128)(2,1)} %q_hbm.1, bf16[1,256,32,128]{3,2,1,0:T(8,128)(2,1)} %do_hbm.1, bf16[4,256,128]{2,1,0:T(8,128)(2,1)} %get-tuple-element.36.bk_ref, ...), custom_call_target="tpu_custom_call" | custom-call | tf_op jit(solution)/shard_map/pallas_call | solution.py:399
  76.4 1.9 %copy.50 = bf16[1,256,4,128]{3,2,1,0:T(4,128)(2,1)} copy(bf16[1,256,4,128]{3,1,2,0:T(8,128)(2,1)} %bitcast.28) | data formatting | bytes 524288
  78.3 0.8 fusion
  79.1 0.6 copy.53
  79.7 0.6 copy.52
  80.3 1.9 %copy.51 = bf16[1,256,4,128]{3,2,1,0:T(4,128)(2,1)} copy(bf16[1,256,4,128]{3,1,2,0:T(8,128)(2,1)} %bitcast.27) | data formatting | bytes 524288
  82.2 3.3 %copy.58 = bf16[1,256,32,128]{3,2,1,0:T(8,128)(2,1)} copy(bf16[1,256,32,128]{3,2,1,0:T(8,128)(2,1)} %get-tuple-element.42) | data formatting | bytes 4194304
  (4 shorter events, 0.0 us)

commit v2 on v1

--- a/solution.py
+++ b/solution.py
@@ -178,14 +178,18 @@
     dv_acc,
     kt_scr,
     gath,
+    own_part,
     send,
+    half,
+    comb,
     recv,
     load_sem,
     store_sem,
+    own_sem,
     gather_sem,
-    own_sem,
-    scatter_send_sem,
-    scatter_recv_sem,
+    pass_sem,
+    half_sem,
+    scatter_sem,
 ):
     branch_count, head_devices, groups, group_size, seq_len, head_dim, pos = dims
     devices = branch_count * head_devices
@@ -194,12 +198,19 @@
     score_scale = scaling * LOG2E
     rows = seq_len * group_size
     wide = 64 * group_size
-    chunk = 256
+    chunk = prompt_len // 2
     early = groups // 2
-    me = lax.axis_index("branch") * head_devices + lax.axis_index("head")
-
-    def ident(index):
-        return (index // head_devices, index % head_devices)
+    chips = branch_count // 2 * head_devices
+    core = lax.axis_index("branch") % 2
+    me = lax.axis_index("branch") // 2 * head_devices + lax.axis_index("head")
+    partner = (lax.axis_index("branch") + 1 - 2 * core, lax.axis_index("head"))
+    far = pl.ds(1, chips - 1)
+
+    def peer(chip):
+        return (chip // head_devices * 2 + core, chip % head_devices)
+
+    def wait_bytes(ref, sem):
+        pltpu.make_async_copy(ref, ref, sem).wait()
 
     def loads(g):
         cut = pl.ds(g * group_size, group_size)
@@ -214,29 +225,77 @@
 
     barrier = pltpu.get_barrier_semaphore()
 
-    @pl.loop(1, devices)
+    @pl.loop(1, chips)
     def _(k):
         pl.semaphore_signal(
-            barrier, inc=1, device_id=ident((me + k) % devices), device_id_type=MESH
-        )
-
+            barrier, inc=1, device_id=peer((me + k) % chips), device_id_type=MESH
+        )
+
+    pl.semaphore_signal(barrier, inc=1, device_id=partner, device_id_type=MESH)
+
+    def own_copy(g):
+        return pltpu.make_async_copy(
+            packed_ref.at[me % head_devices, g], gath.at[g, 0, 0], own_sem.at[g]
+        )
+
+    for g in range(groups):
+        own_copy(g).start()
     dq_acc[...] = jnp.zeros_like(dq_acc)
-    pl.semaphore_wait(barrier, devices - 1)
-
-    @pl.loop(1, devices)
-    def _(k):
-        other = (me + k) % devices
-        pltpu.make_async_remote_copy(
-            src_ref=packed_ref.at[other % head_devices],
-            dst_ref=gath.at[k],
-            send_sem=gather_sem.at[0],
-            recv_sem=gather_sem.at[1],
-            device_id=ident(other),
+    pl.semaphore_wait(barrier, chips)
+
+    @pl.loop(0, groups)
+    def _(g):
+        @pl.loop(1, chips)
+        def _(k):
+            other = (me + k) % chips
+            pltpu.make_async_remote_copy(
+                src_ref=packed_ref.at[other % head_devices, g],
+                dst_ref=gath.at[g, 0, k],
+                send_sem=gather_sem.at[0, g],
+                recv_sem=gather_sem.at[1, g],
+                device_id=peer(other),
+                device_id_type=MESH,
+            ).start()
+
+    def pass_copy(g):
+        return pltpu.make_async_remote_copy(
+            src_ref=gath.at[g, 0],
+            dst_ref=gath.at[g, 1],
+            send_sem=pass_sem.at[0, g],
+            recv_sem=pass_sem.at[1, g],
+            device_id=partner,
             device_id_type=MESH,
-        ).start()
-
-    own = pltpu.make_async_copy(packed_ref.at[me % head_devices], gath.at[0], own_sem)
-    own.start()
+        )
+
+    def pass_on(g):
+        own_copy(g).wait()
+        wait_bytes(gath.at[g, 0, far], gather_sem.at[1, g])
+        pass_copy(g).start()
+
+    def half_copy(g):
+        return pltpu.make_async_remote_copy(
+            src_ref=send.at[g],
+            dst_ref=half.at[g],
+            send_sem=half_sem.at[0, g],
+            recv_sem=half_sem.at[1, g],
+            device_id=partner,
+            device_id_type=MESH,
+        )
+
+    def combine(g):
+        half_copy(g).wait_recv()
+        comb[g] = (own_part[g] + half[g].astype(jnp.float32)).astype(jnp.bfloat16)
+
+        @pl.loop(1, chips)
+        def _(k):
+            pltpu.make_async_remote_copy(
+                src_ref=comb.at[g, k],
+                dst_ref=recv.at[g, k],
+                send_sem=scatter_sem.at[0, g],
+                recv_sem=scatter_sem.at[1, g],
+                device_id=peer((me + chips - k) % chips),
+                device_id_type=MESH,
+            ).start()
 
     def row_block(g, j):
         cut = pl.ds(j * 64, 64)
@@ -269,10 +328,9 @@
         bdv_ref[g] = dv_acc[0:seq_len].astype(jnp.bfloat16)
 
     def prompt_part(g):
-        kt_scr[...] = gath[:, 0, g].reshape(prompt_len, head_dim).T
+        kt_scr[...] = gath[g, :, :, 0].reshape(prompt_len, head_dim).T
         dk_acc[...] = jnp.zeros_like(dk_acc)
         dv_acc[...] = jnp.zeros_like(dv_acc)
-        per = chunk // pos
 
         @pl.loop(0, seq_len // 64)
         def _(j):
@@ -280,8 +338,8 @@
             total = None
             for c in range(prompt_len // chunk):
                 at = slice(c * chunk, (c + 1) * chunk)
-                k = gath[c * per : (c + 1) * per, 0, g].reshape(chunk, head_dim)
-                v = gath[c * per : (c + 1) * per, 1, g].reshape(chunk, head_dim)
+                k = gath[g, c, :, 0].reshape(chunk, head_dim)
+                v = gath[g, c, :, 1].reshape(chunk, head_dim)
                 dq_t, dk, dv = block_terms(
                     q, do, lse, delta, k, v, kt_scr[:, at], None, score_scale
                 )
@@ -290,19 +348,13 @@
                 total = dq_t if total is None else total + dq_t
             dq_acc[g, j] += total
 
-        send[g, :, 0] = (dk_acc[...] * scaling).astype(jnp.bfloat16).reshape(devices, pos, head_dim)
-        send[g, :, 1] = dv_acc[...].astype(jnp.bfloat16).reshape(devices, pos, head_dim)
-
-        @pl.loop(1, devices)
-        def _(k):
-            pltpu.make_async_remote_copy(
-                src_ref=send.at[g, k],
-                dst_ref=recv.at[g, k],
-                send_sem=scatter_send_sem.at[g],
-                recv_sem=scatter_recv_sem.at[g],
-                device_id=ident((me + devices - k) % devices),
-                device_id_type=MESH,
-            ).start()
+        own_part[g, :, 0] = (dk_acc[0:chunk] * scaling).reshape(chips, pos, head_dim)
+        own_part[g, :, 1] = dv_acc[0:chunk].reshape(chips, pos, head_dim)
+        send[g, :, 0] = (
+            (dk_acc[chunk:] * scaling).astype(jnp.bfloat16).reshape(chips, pos, head_dim)
+        )
+        send[g, :, 1] = dv_acc[chunk:].astype(jnp.bfloat16).reshape(chips, pos, head_dim)
+        half_copy(g).start()
 
     def store(g):
         cut = pl.ds(g * group_size, group_size)
@@ -320,10 +372,7 @@
         for copy in loads(g):
             copy.wait()
         branch_part(g)
-
-    own.wait()
-    rest = pl.ds(1, devices - 1)
-    pltpu.make_async_copy(gath.at[rest], gath.at[rest], gather_sem.at[1]).wait()
+        pass_on(g)
 
     @pl.loop(0, groups)
     def _(g):
@@ -332,28 +381,40 @@
             for copy in loads(g):
                 copy.wait()
 
+        pass_copy(g).wait_recv()
         prompt_part(g)
+
+        @pl.when(g + early < groups)
+        def _():
+            pass_on(g + early)
+
+        @pl.when(g > 0)
+        def _():
+            combine(g - 1)
 
     @pl.loop(0, early)
     def _(g):
         finish(g)
+
+    combine(groups - 1)
 
     @pl.loop(early, groups)
     def _(g):
         branch_part(g)
         finish(g)
 
-    pltpu.make_async_copy(gath.at[rest], gath.at[rest], gather_sem.at[0]).wait()
-
     @pl.loop(0, groups)
     def _(g):
-        pltpu.make_async_copy(send.at[g, rest], send.at[g, rest], scatter_send_sem.at[g]).wait()
-        pltpu.make_async_copy(recv.at[g, rest], recv.at[g, rest], scatter_recv_sem.at[g]).wait()
+        wait_bytes(gath.at[g, 0, far], gather_sem.at[0, g])
+        pass_copy(g).wait_send()
+        half_copy(g).wait_send()
+        wait_bytes(comb.at[g, far], scatter_sem.at[0, g])
+        wait_bytes(recv.at[g, far], scatter_sem.at[1, g])
         for apart in range(head_devices):
             owner = (me + apart) % head_devices
             total = None
-            for k in range(apart, devices, head_devices):
-                piece = (send if k == 0 else recv)[g, k].astype(jnp.float32)
+            for k in range(apart, chips, head_devices):
+                piece = (comb if k == 0 else recv)[g, k].astype(jnp.float32)
                 total = piece if total is None else total + piece
             pd_ref[owner, g] = total.astype(jnp.bfloat16)
         store(g).wait()
@@ -377,11 +438,12 @@
     groups = branch_keys.shape[2]
     group_size = head_count // groups
     pos = prompt_keys.shape[0]
-    if pos % 16:
+    if pos % 16 or branch_count % 2:
         return plain_shards(
             queries, grad_out, branch_keys, branch_values, row_lse, row_delta, lengths,
             prompt_keys, prompt_values,
         )
+    chips = devices // 2
     prompt_len = devices * pos
     wide = 64 * group_size
     steps = seq_len // 64
@@ -391,7 +453,7 @@
     rows = rows.reshape(2, groups, group_size, steps, 64)
     rows = rows.transpose(1, 3, 0, 4, 2).reshape(groups, steps, 2, wide)
     packed = jnp.stack([prompt_keys, prompt_values])
-    packed = packed.reshape(2, pos, head_devices, groups, head_dim).transpose(2, 0, 3, 1, 4)
+    packed = packed.reshape(2, pos, head_devices, groups, head_dim).transpose(2, 3, 0, 1, 4)
     dims = (branch_count, head_devices, groups, group_size, seq_len, head_dim, pos)
     vmem = pl.BlockSpec(memory_space=pltpu.VMEM)
     hbm = pl.BlockSpec(memory_space=pl.ANY)
@@ -414,15 +476,19 @@
             pltpu.VMEM((prompt_len, head_dim), full),
             pltpu.VMEM((prompt_len, head_dim), full),
             pltpu.VMEM((head_dim, prompt_len), low),
-            pltpu.VMEM((devices, 2, groups, pos, head_dim), low),
-            pltpu.VMEM((groups, devices, 2, pos, head_dim), low),
-            pltpu.VMEM((groups, devices, 2, pos, head_dim), low),
+            pltpu.VMEM((groups, 2, chips, 2, pos, head_dim), low),
+            pltpu.VMEM((groups, chips, 2, pos, head_dim), full),
+            pltpu.VMEM((groups, chips, 2, pos, head_dim), low),
+            pltpu.VMEM((groups, chips, 2, pos, head_dim), low),
+            pltpu.VMEM((groups, chips, 2, pos, head_dim), low),
+            pltpu.VMEM((groups, chips, 2, pos, head_dim), low),
             pltpu.SemaphoreType.DMA((2, groups)),
             pltpu.SemaphoreType.DMA((groups,)),
-            pltpu.SemaphoreType.DMA((2,)),
-            pltpu.SemaphoreType.DMA,
             pltpu.SemaphoreType.DMA((groups,)),
-            pltpu.SemaphoreType.DMA((groups,)),
+            pltpu.SemaphoreType.DMA((2, groups)),
+            pltpu.SemaphoreType.DMA((2, groups)),
+            pltpu.SemaphoreType.DMA((2, groups)),
+            pltpu.SemaphoreType.DMA((2, groups)),
         ],
         compiler_params=pltpu.CompilerParams(collective_id=0, has_side_effects=True),
     )(

time: 86 us -> 60.8 us (0.71)
  Pallas kernels: 67.8 us -> 42.5 us
    pallas_call x1, Pallas kernels: 67.8 us -> 42.5 us  [shards(): pl.pallas_call(functools.partial(fused_kernel, dims), out_shape=(jax.Shap...]
where the time goes in v2:
time: 60.8 us; the launch traced here: 60.2 us
  Pallas kernels  42.5 us (70%)
  local copies, waits for them, and re-layouts  14.9 us (25%)
  other arithmetic  1.42 us (2%)
  between operations  1.34 us (2%)
    pallas_call x1, Pallas kernels, shards(): pl.pallas_call(functools.partial(fused_kernel, dims), out_shape=(jax.Shap...  42.5 us
    unnamed x7, local copies, waits for them, and re-layouts  9.76 us
    transpose x1, local copies, waits for them, and re-layouts, shards(): branch_values[0].swapaxes(0, 1)  1.89 us

profile of v2, /device:TPU:0, one launch (start us, length us, event | category | flops | bytes accessed | tf_op | source)
XLA Modules:
  0.0 60.2 jit_solution(18246699858657870091)
XLA Ops:
  1.3 0.8 %multiply_select_fusion = f32[1,32,256]{2,1,0:T(8,128)S(1)} fusion(f32[1,32,256]{2,1,0:T(8,128)} %param.13, pred[256]{0:T(512)(128)(4,1)S(1)} %iota_compare_fusion), kind=kLoop, calls=%fused_computation.4 | loop fusion | flops 16384 | bytes 65792 | tf_op jit(solution)/shard_map/jit(_where)/select_n | solution.py:451
  2.1 0.1 stack.17
  2.2 0.8 %copy.48 = bf16[16,8,128]{2,0,1:T(8,128)(2,1)S(1)} copy(bf16[16,8,128]{2,1,0:T(8,128)(2,1)} %param.16) | data formatting | bytes 65536 | tf_op args[7]
  2.9 0.8 %copy.49 = bf16[16,8,128]{2,0,1:T(8,128)(2,1)S(1)} copy(bf16[16,8,128]{2,1,0:T(8,128)(2,1)} %param.17) | data formatting | bytes 65536 | tf_op args[8]
  3.7 0.6 %maximum_bitcast_fusion.1.packed_ref = bf16[2,4,2,16,128]{4,3,2,1,0:T(8,128)(2,1)} fusion(bf16[1,16,2,4,128]{4,1,0,3,2:T(8,128)(2,1)S(1)} %bitcast.32, bf16[1,16,2,4,128]{4,1,0,3,2:T(8,128)(2,1)S(1)} %bitcast.31), kind=kLoop, calls=%fused_computation.3 | loop fusion | flops 32768 | bytes 131072 | tf_op jit(solution)/shard_map/transpose | solution.py:456
  4.3 0.8 %stack.18 = f32[1,4,8,4,64]{4,3,2,1,0:T(4,128)S(1)} reshape(f32[1,32,256]{2,1,0:T(8,128)} %param.14) | data formatting | bytes 65536 | tf_op jit(solution)/shard_map/stack | solution.py:452
  5.2 1.9 %copy_bitcast_fusion = (bf16[4,256,128]{2,1,0:T(8,128)(2,1)}, bf16[4,256,128]{2,1,0:T(8,128)(2,1)}) fusion(bf16[1,256,4,128]{3,2,1,0:T(4,128)(2,1)} %param.12, bf16[1,256,4,128]{3,2,1,0:T(4,128)(2,1)} %param.11), kind=kLoop, calls=%fused_computation | loop fusion | bytes 1048576 | tf_op jit(solution)/shard_map/transpose | solution.py:498
  7.1 0.3 copy.47
  7.5 1.2 %reshape.31.rows_ref = f32[4,4,2,512]{3,2,1,0:T(2,128)} reshape(f32[4,4,2,64,8]{4,3,2,1,0:T(8,128)S(1)} %copy.47) | data formatting | bytes 131072 | tf_op jit(solution)/shard_map/reshape | solution.py:454
  8.6 42.5 %shard_map.128 = (bf16[1,256,32,128]{3,2,1,0:T(8,128)(2,1)}, bf16[4,256,128]{2,1,0:T(8,128)(2,1)}, bf16[4,256,128]{2,1,0:T(8,128)(2,1)}, bf16[2,4,2,16,128]{4,3,2,1,0:T(8,128)(2,1)}) custom-call(bf16[1,256,32,128]{3,2,1,0:T(8,128)(2,1)} %q_hbm.1, bf16[1,256,32,128]{3,2,1,0:T(8,128)(2,1)} %do_hbm.1, bf16[4,256,128]{2,1,0:T(8,128)(2,1)} %get-tuple-element.36.bk_ref, ...), custom_call_target="tpu_custom_call" | custom-call | tf_op jit(solution)/shard_map/pallas_call | solution.py:461
  51.2 1.9 %copy.50 = bf16[1,256,4,128]{3,2,1,0:T(4,128)(2,1)} copy(bf16[1,256,4,128]{3,1,2,0:T(8,128)(2,1)} %bitcast.28) | data formatting | bytes 524288
  53.0 0.8 %fusion = (bf16[1,16,2,4,128]{4,1,0,3,2:T(8,128)(2,1)S(1)}, bf16[1,16,2,4,128]{4,1,0,3,2:T(8,128)(2,1)S(1)}) fusion(bf16[2,16,2,4,128]{4,1,0,3,2:T(8,128)(2,1)} %bitcast.33), kind=kLoop, calls=%fused_computation.6 | loop fusion | bytes 131072 | tf_op jit(solution)/shard_map/slice | solution.py:503
  53.8 0.6 %copy.53 = bf16[16,8,128]{2,1,0:T(8,128)(2,1)} copy(bf16[16,8,128]{2,0,1:T(8,128)(2,1)S(1)} %bitcast.30) | data formatting | bytes 65536
  54.4 0.6 %copy.52 = bf16[16,8,128]{2,1,0:T(8,128)(2,1)} copy(bf16[16,8,128]{2,0,1:T(8,128)(2,1)S(1)} %bitcast.29) | data formatting | bytes 65536
  55.1 1.9 %copy.51 = bf16[1,256,4,128]{3,2,1,0:T(4,128)(2,1)} copy(bf16[1,256,4,128]{3,1,2,0:T(8,128)(2,1)} %bitcast.27) | data formatting | bytes 524288
  56.9 3.3 %copy.58 = bf16[1,256,32,128]{3,2,1,0:T(8,128)(2,1)} copy(bf16[1,256,32,128]{3,2,1,0:T(8,128)(2,1)} %get-tuple-element.42) | data formatting | bytes 4194304
  (4 shorter events, 0.0 us)
